TPU v7x, 32 devices: a whole 2x2x4 slice. The times are simulated.
32 devices in a mesh: ctx: 8 (over z, core), head: 4 (over y, x).
Axes of the slice: x: 2, y: 2, z: 4, core: 2. Of those that a mesh axis runs over, the one named last changes fastest.
Arguments:
- q_latent: bfloat16 [1024, 128, 512], P('ctx', 'head'), may hold values from -4 to 4
- q_rope: bfloat16 [1024, 8192], P('ctx', 'head'), may hold values from -5 to 5
- latent: bfloat16 [1024, 512], P('ctx'), may hold values from -5 to 5
- key_rope: bfloat16 [1024, 64], P('ctx'), may hold values from -5 to 5
- out_grad: bfloat16 [1024, 128, 512], P('ctx', 'head'), may hold values from -5 to 5
- inputs: bfloat16 [1024, 7168], P('ctx', 'head'), may hold values from -5 to 5
- doc_ids: int32 [1024], replicated, may hold values from 0 to 7, never falling along the last dimension, each value on 1 to 256 neighbouring positions
Outputs:
- q_latent_grad: bfloat16 [1024, 128, 512], P('ctx', 'head')
- q_rope_grad: bfloat16 [1024, 8192], P('ctx', 'head')
- latent_grad: bfloat16 [1024, 512], P('ctx')
- key_rope_grad: bfloat16 [1024, 64], P('ctx')
- proj_grad: float32 [512, 7168], P('ctx', 'head')
Inputs may be any that keep to these rules, and one draw needn't show every extreme that they name: `doc_ids`: ids never fall along the sequence; each document has at most 256 positions.
All inputs are finite; a program needn't handle non-finite values.
Results may differ from a plain program's by a relative error of at most 0.0058.
Values may be sent and summed in bfloat16 or wider, within the bound.
No kernel may reach another device: no remote copies, remote signals or barrier semaphores. Data moves between devices by JAX's collectives and lax.ppermute only.
A program may use at most 128 MiB of HBM per device.

v0:
```python
import jax
import jax.numpy as jnp
from jax import lax
from jax.sharding import PartitionSpec as P

WIN_BLK = 3
softmax_scale = 192.0 ** (-0.5)


def passed_along(array, axis, by):
    peers = lax.axis_size(axis)
    pairs = [(i, i + by) for i in range(peers) if 0 <= i + by < peers]
    return lax.ppermute(array, axis, pairs)


def shards(q_latent, q_rope, latent, key_rope, out_grad, inputs, doc_ids):
    tok = latent.shape[0]
    heads_here = q_latent.shape[1]
    rope_width = key_rope.shape[1]
    lat_width = latent.shape[1]
    depth = WIN_BLK
    window = depth * tok
    rank = lax.axis_index("ctx")
    earlier = []
    for back in range(depth, 0, -1):
        earlier.append(passed_along((latent, key_rope), "ctx", back))
    keys_lat = jnp.concatenate([pair[0] for pair in earlier] + [latent], axis=0)
    keys_rope = jnp.concatenate([pair[1] for pair in earlier] + [key_rope], axis=0)
    start = rank * tok
    doc_pad = jnp.concatenate([jnp.full((window,), -1, jnp.int32), doc_ids], axis=0)
    key_doc = lax.dynamic_slice_in_dim(doc_pad, start, window + tok, 0)
    query_doc = lax.dynamic_slice_in_dim(doc_ids, start, tok, 0)
    qpos = jnp.arange(tok, dtype=jnp.int32)
    kpos = jnp.arange(window + tok, dtype=jnp.int32) - window
    allowed = (
        (kpos[None, :] <= qpos[:, None])
        & (qpos[:, None] - kpos[None, :] < window)
        & (key_doc[None, :] == query_doc[:, None])
    )
    qrope_heads = q_rope.reshape(tok, heads_here, rope_width)
    scores = (
        jnp.einsum("thj,kj->thk", q_latent, keys_lat, preferred_element_type=jnp.float32)
        + jnp.einsum("thr,kr->thk", qrope_heads, keys_rope, preferred_element_type=jnp.float32)
    ) * softmax_scale
    masked = jnp.where(allowed[:, None, :], scores, -jnp.inf)
    top = jnp.max(masked, axis=-1, keepdims=True)
    expo = jnp.exp(masked - top)
    probs = expo / jnp.sum(expo, axis=-1, keepdims=True)
    probs_low = probs.astype(jnp.bfloat16)
    merged = jnp.einsum("thk,kj->thj", probs_low, keys_lat, preferred_element_type=jnp.float32)
    delta = jnp.sum(out_grad * merged, axis=-1)
    dprob = jnp.einsum("thj,kj->thk", out_grad, keys_lat, preferred_element_type=jnp.float32)
    dscore = (probs * (dprob - delta[..., None]) * softmax_scale).astype(jnp.bfloat16)
    q_latent_grad = jnp.einsum(
        "thk,kj->thj", dscore, keys_lat, preferred_element_type=jnp.float32
    ).astype(jnp.bfloat16)
    q_rope_grad = jnp.einsum("thk,kr->thr", dscore, keys_rope, preferred_element_type=jnp.float32)
    q_rope_grad = q_rope_grad.reshape(tok, heads_here * rope_width).astype(jnp.bfloat16)
    part_lat = jnp.einsum(
        "thk,thj->kj", dscore, q_latent, preferred_element_type=jnp.float32
    ) + jnp.einsum("thk,thj->kj", probs_low, out_grad, preferred_element_type=jnp.float32)
    part_rope = jnp.einsum("thk,thr->kr", dscore, qrope_heads, preferred_element_type=jnp.float32)
    blocks_lat = part_lat.reshape(depth + 1, tok, lat_width)
    blocks_rope = part_rope.reshape(depth + 1, tok, rope_width)
    share_lat, share_rope = (
        lax.psum_scatter(blocks_lat, "head", scatter_dimension=1, tiled=True),
        lax.psum_scatter(blocks_rope, "head", scatter_dimension=1, tiled=True),
    )
    own_lat = share_lat[depth]
    own_rope = share_rope[depth]
    for back in range(1, depth + 1):
        got_lat, got_rope = passed_along(
            (share_lat[depth - back], share_rope[depth - back]), "ctx", -back
        )
        own_lat = own_lat + got_lat
        own_rope = own_rope + got_rope
    latent_grad, key_rope_grad = (
        lax.all_gather(own_lat.astype(jnp.bfloat16), "head", axis=0, tiled=True),
        lax.all_gather(own_rope.astype(jnp.bfloat16), "head", axis=0, tiled=True),
    )
    proj_grad = lax.psum_scatter(
        lax.dot_general(
            latent_grad, inputs, (((0,), (0,)), ((), ())), preferred_element_type=jnp.float32
        ),
        "ctx",
        scatter_dimension=0,
        tiled=True,
    )
    return (q_latent_grad, q_rope_grad, latent_grad, key_rope_grad, proj_grad)


def solution(mesh):
    placed = (
        P("ctx", "head", None),
        P("ctx", "head"),
        P("ctx", None),
        P("ctx", None),
        P("ctx", "head", None),
        P("ctx", "head"),
        P(),
    )
    return jax.shard_map(
        shards,
        mesh=mesh,
        in_specs=placed,
        out_specs=(
            P("ctx", "head", None),
            P("ctx", "head"),
            P("ctx", None),
            P("ctx", None),
            P("ctx", "head"),
        ),
        check_vma=False,
    )
```

profile of v0, /device:TPU:0, one launch (start us, length us, event | category | flops | bytes accessed | tf_op | source)
XLA Modules:
  0.0 199.9 jit_solution(8502988981172908835)
XLA Ops:
  7.2 4.5 %collective-permute-start.3 = (bf16[128,64]{0,1:T(8,128)(2,1)}, bf16[128,64]{0,1:T(8,128)(2,1)S(1)}, u32[]{:S(2)}, u32[]{:S(2)}) collective-permute-start(bf16[128,64]{0,1:T(8,128)(2,1)} %param.10), channel_id=1, source_target_pairs={{0,12},{4,16},{8,20},{12,24},{16,28},{1,13},{5,17},{9,21},{13,25},... | collective-permute-start | bytes 49160 | tf_op jit(solution)/shard_map/ppermute | solution.py:13
  11.8 3.5 %collective-permute-start.4 = (bf16[128,64]{0,1:T(8,128)(2,1)}, bf16[128,64]{0,1:T(8,128)(2,1)S(1)}, u32[]{:S(2)}, u32[]{:S(2)}) collective-permute-start(bf16[128,64]{0,1:T(8,128)(2,1)} %param.10), channel_id=1, source_target_pairs={{0,8},{4,12},{8,16},{12,20},{16,24},{20,28},{1,9},{5,13},{9,17},{1... | collective-permute-start | bytes 49160 | tf_op jit(solution)/shard_map/ppermute | solution.py:13
  15.3 3.3 %collective-permute-start.5 = (bf16[128,64]{0,1:T(8,128)(2,1)}, bf16[128,64]{0,1:T(8,128)(2,1)S(1)}, u32[]{:S(2)}, u32[]{:S(2)}) collective-permute-start(bf16[128,64]{0,1:T(8,128)(2,1)} %param.10), channel_id=1, source_target_pairs={{0,4},{4,8},{8,12},{12,16},{16,20},{20,24},{24,28},{1,5},{5,9},{9,... | collective-permute-start | bytes 49160 | tf_op jit(solution)/shard_map/ppermute | solution.py:13
  18.6 1.8 collective-permute-start
  20.4 1.7 collective-permute-start.1
  22.1 0.8 pad_dynamic-slice_fusion
  22.9 0.8 dynamic_slice.7
  23.7 0.2 fusion.34
  23.9 1.3 copy.27
  25.2 2.3 %collective-permute-start.2 = (bf16[128,512]{1,0:T(8,128)(2,1)}, bf16[128,512]{1,0:T(8,128)(2,1)S(1)}, u32[]{:S(2)}, u32[]{:S(2)}) collective-permute-start(bf16[128,512]{1,0:T(8,128)(2,1)} %param.9), channel_id=1, source_target_pairs={{0,4},{4,8},{8,12},{12,16},{16,20},{20,24},{24,28},{1,5},{5,9},{9,... | collective-permute-start | bytes 393224 | tf_op jit(solution)/shard_map/ppermute | solution.py:13
  27.5 2.0 fusion.41
  29.5 9.6 %fusion.7 = (f32[128,32]{0,1:T(8,128)S(1)}, f32[512,128,32]{1,0,2:T(8,128)S(1)}) fusion(pred[128,512]{0,1:T(8,128)(4,1)S(1)} %fusion.34, f32[512,128,32]{1,0,2:T(8,128)S(1)} %fusion.41, bf16[128,32,512]{2,1,0:T(8,128)(2,1)} %param.7, bf16[128,512]{1,0:T(8,128)(2,1)S(1)} %copy-done.3, bf16[128,512]{1,0:T(8,128)(2,1)S(1)} %collective-permute-done.2, ...), kind=kOutput, calls=%fused_computation.14 | convolution fusion | flops 2157965312 | bytes 21577728 | tf_op jit(solution)/shard_map/thj,kj->thk/dot_general | solution.py:42
  39.1 1.6 fusion.9
  40.8 3.6 %copy-done.5 = bf16[128,32,512]{2,1,0:T(8,128)(2,1)S(1)} copy-done((bf16[128,32,512]{2,1,0:T(8,128)(2,1)S(1)}, bf16[128,32,512]{2,1,0:T(8,128)(2,1)}, u32[]{:S(2)}) %copy-start.5) | copy-done | bytes 4194328
  44.4 7.6 %fusion.22 = f32[512,512]{1,0:T(8,128)S(1)} fusion(bf16[128,32,512]{2,1,0:T(8,128)(2,1)S(1)} %copy-done.5, f32[512,128,32]{1,0,2:T(8,128)S(1)} %get-tuple-element.22, f32[128,32]{0,1:T(8,128)S(1)} %fusion.9, f32[128,32]{0,1:T(8,128)S(1)} %get-tuple-element.21, pred[128,512]{0,1:T(8,128)(4,1)S(1)} %fusion.34), kind=kOutput, calls=%fused_computation.28 | convolution fusion | flops 2155872256 | bytes 13729792 | tf_op jit(solution)/shard_map/thk,thj->kj/dot_general | solution.py:61
  52.0 7.4 %multiply_reduce_fusion = f32[128,32]{0,1:T(8,128)S(1)} fusion(bf16[128,32,512]{2,1,0:T(8,128)(2,1)S(1)} %copy-done.5, bf16[128,512]{1,0:T(8,128)(2,1)S(1)} %copy-done.3, bf16[128,512]{1,0:T(8,128)(2,1)S(1)} %collective-permute-done.2, bf16[128,512]{1,0:T(8,128)(2,1)S(1)} %collective-permute-done.1, bf16[128,512]{1,0:T(8,128)(2,1)S(1)} %collective-permute-done, ...), kind=kOutput, calls=%fused_computation.11 | convolution fusion | flops 2164256768 | bytes 13221888 | tf_op jit(solution)/shard_map/thk,kj->thj/dot_general | solution.py:50
  59.4 10.1 %fusion.6 = (bf16[128,32,512]{0,2,1:T(8,128)(2,1)S(1)}, f32[512,128,32]{1,0,2:T(8,128)}) fusion(f32[128,32]{0,1:T(8,128)S(1)} %multiply_reduce_fusion, f32[128,32]{0,1:T(8,128)S(1)} %fusion.9, f32[128,32]{0,1:T(8,128)S(1)} %get-tuple-element.21, f32[512,128,32]{1,0,2:T(8,128)S(1)} %get-tuple-element.22, pred[128,512]{0,1:T(8,128)(4,1)S(1)} %fusion.34, ...), kind=kOutput, calls=%fused_computation.9 | convolution fusion | flops 2164260864 | bytes 25804800 | tf_op jit(solution)/shard_map/thj,kj->thk/dot_general | solution.py:52
  69.6 2.0 %copy-done.2 = bf16[128,32,512]{0,2,1:T(8,128)(2,1)} copy-done((bf16[128,32,512]{0,2,1:T(8,128)(2,1)}, bf16[128,32,512]{0,2,1:T(8,128)(2,1)S(1)}, u32[]{:S(2)}) %copy-start.2) | copy-done | bytes 4194328
  71.6 8.3 %fusion.30 = f32[512,512]{1,0:T(8,128)} fusion(f32[512,512]{1,0:T(8,128)S(1)} %fusion.22, bf16[128,32,512]{0,2,1:T(8,128)(2,1)S(1)} %get-tuple-element.23, bf16[128,32,512]{2,1,0:T(8,128)(2,1)} %param.7), kind=kOutput, calls=%fused_computation.30 | convolution fusion | flops 2147745792 | bytes 10485760 | tf_op jit(solution)/shard_map/thk,thj->kj/dot_general | solution.py:59
  79.9 0.0 reduce-scatter.6.cloned.1.call-start
  80.0 0.2 fusion.36
  80.2 8.6 %fusion.2 = bf16[512,32,128]{2,0,1:T(8,128)(2,1)} fusion(f32[512,128,32]{1,0,2:T(8,128)} %get-tuple-element.24, f32[512,128,32]{1,0,2:T(8,128)} %copy-done.1, f32[32,128]{1,0:T(8,128)S(1)} %bitcast.120, f32[32,128]{1,0:T(8,128)S(1)} %bitcast.119, f32[32,128]{1,0:T(8,128)S(1)} %bitcast.118, pred[512,128]{1,0:T(8,128)(4,1)S(1)} %fusion.36), kind=kLoop, calls=%fused_computation.3 | loop fusion | flops 14680064 | bytes 21086208 | tf_op jit(solution)/shard_map/convert_element_type | solution.py:53
  88.8 19.6 %reduce-scatter.4.cloned.1.call-done = f32[4,32,512]{2,1,0:T(8,128)} async-done(((f32[4,128,512]{2,1,0:T(8,128)}), f32[4,32,512]{2,1,0:T(8,128)}) %reduce-scatter.4.cloned.1.call-update) | async-done | bytes 262160 | tf_op jit(solution)/shard_map/reduce_scatter | solution.py:66
  108.3 0.9 slice_bitcast_fusion.2
  109.2 1.3 collective-permute-start.6
  110.5 1.3 collective-permute-start.7
  111.8 1.3 collective-permute-start.8
  113.1 4.1 %convolution_bitcast_fusion = f32[4,128,64]{2,1,0:T(8,128)} fusion(bf16[4,128,32,128]{3,1,0,2:T(8,128)(2,1)} %bitcast.113, bf16[128,32,64,1]{0,2,3,1:T(8,128)(2,1)S(1)} %bitcast.115), kind=kOutput, calls=%fused_computation.32 | convolution fusion | flops 268435456 | bytes 4849664 | tf_op jit(solution)/shard_map/thk,thr->kr/dot_general | solution.py:62
  117.3 0.0 reduce-scatter.8.cloned.1.call-start
  117.4 0.1 collective-permute-done.7
  117.4 1.4 collective-permute-done.8
  118.8 0.9 fusion.40
  119.7 8.4 %all_gather.6 = bf16[128,512]{1,0:T(8,128)(2,1)S(1)} all-gather(bf16[32,512]{1,0:T(8,128)(2,1)S(1)} %fusion.40), channel_id=1, replica_groups=mesh['ctx'=8,'head'=4] {'head'}, dimensions={0}, use_global_device_ids=true | all-gather | bytes 163840 | tf_op jit(solution)/shard_map/all_gather | solution.py:78
  128.1 2.5 %fusion.50 = f32[512,1792]{1,0:T(8,128)} fusion(bf16[128,512]{1,0:T(8,128)(2,1)S(1)} %all_gather.6, bf16[128,1792]{1,0:T(8,128)(2,1)S(1)} %copy-done), kind=kOutput, calls=%fused_computation.64 | convolution fusion | flops 234881024 | bytes 4259840 | tf_op jit(solution)/shard_map/dot_general | solution.py:82
  130.6 6.5 %convolution_convert_fusion = bf16[128,32,512]{2,0,1:T(8,128)(2,1)} fusion(bf16[128,32,512]{0,2,1:T(8,128)(2,1)} %copy-done.2, bf16[128,512]{1,0:T(8,128)(2,1)S(1)} %copy-done.3, bf16[128,512]{1,0:T(8,128)(2,1)S(1)} %collective-permute-done.2, bf16[128,512]{1,0:T(8,128)(2,1)S(1)} %collective-permute-done.1, bf16[128,512]{1,0:T(8,128)(2,1)S(1)} %collective-permute-done), kind=kOutput, calls=%fused_computation.25 | convolution fusion | flops 2151677952 | bytes 8912896 | tf_op jit(solution)/shard_map/thk,kj->thj/dot_general | solution.py:54
  137.1 7.4 %reduce-scatter.6.cloned.1.call-done = f32[4,32,64]{2,1,0:T(8,128)} async-done(((f32[4,128,64]{2,1,0:T(8,128)}), f32[4,32,64]{2,1,0:T(8,128)}) %reduce-scatter.6.cloned.1.call-update) | async-done | bytes 32784 | tf_op jit(solution)/shard_map/reduce_scatter | solution.py:67
  144.5 0.8 slice_bitcast_fusion.6
  145.3 1.3 collective-permute-start.10
  146.6 1.3 collective-permute-start.11
  147.9 1.6 collective-permute-start.9
  149.5 3.0 %convolution_convert_fusion.1 = bf16[128,32,64]{0,2,1:T(8,128)(2,1)S(1)} fusion(bf16[128,32,512]{0,2,1:T(8,128)(2,1)} %copy-done.2, bf16[128,64]{0,1:T(8,128)(2,1)S(1)} %copy-done.4, bf16[128,64]{0,1:T(8,128)(2,1)S(1)} %collective-permute-done.5, bf16[128,64]{0,1:T(8,128)(2,1)S(1)} %collective-permute-done.4, bf16[128,64]{0,1:T(8,128)(2,1)S(1)} %collective-permute-done.3), kind=kOutput, calls=%fused_computation.31 | convolution fusion | flops 268959744 | bytes 4784128 | tf_op jit(solution)/shard_map/thk,kr->thr/dot_general | solution.py:57
  152.5 6.9 %copy.36 = bf16[128,32,512]{2,1,0:T(8,128)(2,1)} copy(bf16[128,32,512]{2,0,1:T(8,128)(2,1)} %convolution_convert_fusion) | data formatting | bytes 8388608
  159.4 1.0 copy.37
  160.4 0.7 fusion.45
  161.1 8.2 %all_gather.7 = bf16[128,64]{1,0:T(8,128)(2,1)S(1)} all-gather(bf16[32,64]{1,0:T(8,128)(2,1)S(1)} %fusion.45), channel_id=1, replica_groups=mesh['ctx'=8,'head'=4] {'head'}, dimensions={0}, use_global_device_ids=true | all-gather | bytes 20480 | tf_op jit(solution)/shard_map/all_gather | solution.py:79
  169.3 0.7 copy.38
  170.0 22.7 %reduce-scatter.8.cloned.1.call-done = f32[64,1792]{1,0:T(8,128)} async-done(((f32[512,1792]{1,0:T(8,128)}), f32[64,1792]{1,0:T(8,128)}) %reduce-scatter.8.cloned.1.call-update) | async-done | bytes 458768 | tf_op jit(solution)/shard_map/reduce_scatter | solution.py:81
  192.7 0.7 copy.66
  (24 shorter events, 0.1 us)
Async XLA Ops:
  7.2 120.9 %copy-start = (bf16[128,1792]{1,0:T(8,128)(2,1)S(1)}, bf16[128,1792]{1,0:T(8,128)(2,1)}, u32[]{:S(2)}) copy-start(bf16[128,1792]{1,0:T(8,128)(2,1)} %param.12) | copy-start | bytes 1376260
  7.2 22.3 %copy-start.3 = (bf16[128,512]{1,0:T(8,128)(2,1)S(1)}, bf16[128,512]{1,0:T(8,128)(2,1)}, u32[]{:S(2)}) copy-start(bf16[128,512]{1,0:T(8,128)(2,1)} %param.9) | copy-start | bytes 393220
  7.2 101.1 %reduce-scatter.4.cloned.1.call-start = ((), (), s32[]{:S(2)}) async-start(), calls=%async_computation.3 | async-start | bytes 1310720 | tf_op jit(solution)/shard_map/reduce_scatter | solution.py:66
  7.2 18.0 %collective-permute-start.3 = (bf16[128,64]{0,1:T(8,128)(2,1)}, bf16[128,64]{0,1:T(8,128)(2,1)S(1)}, u32[]{:S(2)}, u32[]{:S(2)}) collective-permute-start(bf16[128,64]{0,1:T(8,128)(2,1)} %param.10), channel_id=1, source_target_pairs={{0,12},{4,16},{8,20},{12,24},{16,28},{1,13},{5,17},{9,21},{13,25},... | collective-permute-start | bytes 49160 | tf_op jit(solution)/shard_map/ppermute | solution.py:13
  11.8 15.7 %collective-permute-start.4 = (bf16[128,64]{0,1:T(8,128)(2,1)}, bf16[128,64]{0,1:T(8,128)(2,1)S(1)}, u32[]{:S(2)}, u32[]{:S(2)}) collective-permute-start(bf16[128,64]{0,1:T(8,128)(2,1)} %param.10), channel_id=1, source_target_pairs={{0,8},{4,12},{8,16},{12,20},{16,24},{20,28},{1,9},{5,13},{9,17},{1... | collective-permute-start | bytes 49160 | tf_op jit(solution)/shard_map/ppermute | solution.py:13
  15.3 12.2 %collective-permute-start.5 = (bf16[128,64]{0,1:T(8,128)(2,1)}, bf16[128,64]{0,1:T(8,128)(2,1)S(1)}, u32[]{:S(2)}, u32[]{:S(2)}) collective-permute-start(bf16[128,64]{0,1:T(8,128)(2,1)} %param.10), channel_id=1, source_target_pairs={{0,4},{4,8},{8,12},{12,16},{16,20},{20,24},{24,28},{1,5},{5,9},{9,... | collective-permute-start | bytes 49160 | tf_op jit(solution)/shard_map/ppermute | solution.py:13
  18.6 10.9 %collective-permute-start = (bf16[128,512]{1,0:T(8,128)(2,1)}, bf16[128,512]{1,0:T(8,128)(2,1)S(1)}, u32[]{:S(2)}, u32[]{:S(2)}) collective-permute-start(bf16[128,512]{1,0:T(8,128)(2,1)} %param.9), channel_id=1, source_target_pairs={{0,12},{4,16},{8,20},{12,24},{16,28},{1,13},{5,17},{9,21},{13,25},... | collective-permute-start | bytes 393224 | tf_op jit(solution)/shard_map/ppermute | solution.py:13
  20.4 9.1 %collective-permute-start.1 = (bf16[128,512]{1,0:T(8,128)(2,1)}, bf16[128,512]{1,0:T(8,128)(2,1)S(1)}, u32[]{:S(2)}, u32[]{:S(2)}) collective-permute-start(bf16[128,512]{1,0:T(8,128)(2,1)} %param.9), channel_id=1, source_target_pairs={{0,8},{4,12},{8,16},{12,20},{16,24},{20,28},{1,9},{5,13},{9,17},{1... | collective-permute-start | bytes 393224 | tf_op jit(solution)/shard_map/ppermute | solution.py:13
  25.2 4.3 %collective-permute-start.2 = (bf16[128,512]{1,0:T(8,128)(2,1)}, bf16[128,512]{1,0:T(8,128)(2,1)S(1)}, u32[]{:S(2)}, u32[]{:S(2)}) collective-permute-start(bf16[128,512]{1,0:T(8,128)(2,1)} %param.9), channel_id=1, source_target_pairs={{0,4},{4,8},{8,12},{12,16},{16,20},{20,24},{24,28},{1,5},{5,9},{9,... | collective-permute-start | bytes 393224 | tf_op jit(solution)/shard_map/ppermute | solution.py:13
  39.1 20.3 %copy-start.1 = (f32[512,128,32]{1,0,2:T(8,128)}, f32[512,128,32]{1,0,2:T(8,128)S(1)}, u32[]{:S(2)}) copy-start(f32[512,128,32]{1,0,2:T(8,128)S(1)} %get-tuple-element.22) | copy-start | bytes 25165828
  39.1 5.2 %copy-start.5 = (bf16[128,32,512]{2,1,0:T(8,128)(2,1)S(1)}, bf16[128,32,512]{2,1,0:T(8,128)(2,1)}, u32[]{:S(2)}) copy-start(bf16[128,32,512]{2,1,0:T(8,128)(2,1)} %param.11) | copy-start | bytes 12582916
  69.5 2.0 %copy-start.2 = (bf16[128,32,512]{0,2,1:T(8,128)(2,1)}, bf16[128,32,512]{0,2,1:T(8,128)(2,1)S(1)}, u32[]{:S(2)}) copy-start(bf16[128,32,512]{0,2,1:T(8,128)(2,1)S(1)} %get-tuple-element.23) | copy-start | bytes 12582916
  79.9 64.6 %reduce-scatter.6.cloned.1.call-start = ((), (), s32[]{:S(2)}) async-start(), calls=%async_computation.4 | async-start | bytes 327680 | tf_op jit(solution)/shard_map/reduce_scatter | solution.py:67
  109.2 8.1 %collective-permute-start.6 = (f32[32,512]{1,0:T(8,128)S(1)}, f32[32,512]{1,0:T(8,128)S(1)}, u32[]{:S(2)}, u32[]{:S(2)}) collective-permute-start(f32[32,512]{1,0:T(8,128)S(1)} %get-tuple-element.15), channel_id=1, source_target_pairs={{4,0},{8,4},{12,8},{16,12},{20,16},{24,20},{28,24},{5,1},{9,5},{13... | collective-permute-start | bytes 196616 | tf_op jit(solution)/shard_map/ppermute | solution.py:13
  110.5 6.9 %collective-permute-start.7 = (f32[32,512]{1,0:T(8,128)S(1)}, f32[32,512]{1,0:T(8,128)S(1)}, u32[]{:S(2)}, u32[]{:S(2)}) collective-permute-start(f32[32,512]{1,0:T(8,128)S(1)} %get-tuple-element.17), channel_id=1, source_target_pairs={{8,0},{12,4},{16,8},{20,12},{24,16},{28,20},{9,1},{13,5},{17,9},{2... | collective-permute-start | bytes 196616 | tf_op jit(solution)/shard_map/ppermute | solution.py:13
  111.8 6.9 %collective-permute-start.8 = (f32[32,512]{1,0:T(8,128)S(1)}, f32[32,512]{1,0:T(8,128)S(1)}, u32[]{:S(2)}, u32[]{:S(2)}) collective-permute-start(f32[32,512]{1,0:T(8,128)S(1)} %get-tuple-element.16), channel_id=1, source_target_pairs={{12,0},{16,4},{20,8},{24,12},{28,16},{13,1},{17,5},{21,9},{25,13},... | collective-permute-start | bytes 196616 | tf_op jit(solution)/shard_map/ppermute | solution.py:13
  117.3 75.4 %reduce-scatter.8.cloned.1.call-start = ((), (), s32[]{:S(2)}) async-start(), calls=%async_computation.5 | async-start | bytes 4128768 | tf_op jit(solution)/shard_map/reduce_scatter | solution.py:81
  128.1 21.4 %copy-start.4 = (bf16[128,64]{0,1:T(8,128)(2,1)S(1)}, bf16[128,64]{0,1:T(8,128)(2,1)}, u32[]{:S(2)}) copy-start(bf16[128,64]{0,1:T(8,128)(2,1)} %param.10) | copy-start | bytes 49156
  145.3 15.1 %collective-permute-start.10 = (f32[32,64]{1,0:T(8,128)S(1)}, f32[32,64]{1,0:T(8,128)S(1)}, u32[]{:S(2)}, u32[]{:S(2)}) collective-permute-start(f32[32,64]{1,0:T(8,128)S(1)} %get-tuple-element.20), channel_id=1, source_target_pairs={{8,0},{12,4},{16,8},{20,12},{24,16},{28,20},{9,1},{13,5},{17,9},{2... | collective-permute-start | bytes 24584 | tf_op jit(solution)/shard_map/ppermute | solution.py:13
  146.6 13.8 %collective-permute-start.11 = (f32[32,64]{1,0:T(8,128)S(1)}, f32[32,64]{1,0:T(8,128)S(1)}, u32[]{:S(2)}, u32[]{:S(2)}) collective-permute-start(f32[32,64]{1,0:T(8,128)S(1)} %get-tuple-element.19), channel_id=1, source_target_pairs={{12,0},{16,4},{20,8},{24,12},{28,16},{13,1},{17,5},{21,9},{25,13},... | collective-permute-start | bytes 24584 | tf_op jit(solution)/shard_map/ppermute | solution.py:13
  147.9 12.5 %collective-permute-start.9 = (f32[32,64]{1,0:T(8,128)S(1)}, f32[32,64]{1,0:T(8,128)S(1)}, u32[]{:S(2)}, u32[]{:S(2)}) collective-permute-start(f32[32,64]{1,0:T(8,128)S(1)} %get-tuple-element.18), channel_id=1, source_target_pairs={{4,0},{8,4},{12,8},{16,12},{20,16},{24,20},{28,24},{5,1},{9,5},{13... | collective-permute-start | bytes 24584 | tf_op jit(solution)/shard_map/ppermute | solution.py:13
Sparse Core Ops, SparseCore 0:
  80.0 28.2 reduce-scatter.3
  117.4 27.0 reduce-scatter.5
  147.4 45.2 reduce-scatter.7
where the time goes:
time: 201 us; the launch traced here: 200 us
  matrix products  61.2 us (30%)
  waiting for transfers between devices  51.3 us (26%)
  starting transfers between devices  25.2 us (13%)
  local copies, waits for them, and re-layouts  18.6 us (9%)
  blocking collectives  16.6 us (8%)
  between operations  14 us (7%)
  other arithmetic  13 us (6%)
    ppermute x12, starting transfers between devices, passed_along(): return lax.ppermute(array, axis, pairs)  25.1 us
    reduce_scatter x1, waiting for transfers between devices, shards(): lax.psum_scatter(lax.dot_general(latent_grad, inputs, (((0,), (0,)), ((),...  22.7 us
    reduce_scatter x1, waiting for transfers between devices, shards(): lax.psum_scatter(blocks_lat, 'head', scatter_dimension=1, tiled=True)  19.6 us
    unnamed x17, local copies, waits for them, and re-layouts  16.2 us
    dot_general x1, matrix products, shards(): jnp.einsum('thj,kj->thk', out_grad, keys_lat, preferred_element_type=jnp....  10.1 us
    dot_general x1, matrix products, shards(): jnp.einsum('thj,kj->thk', q_latent, keys_lat, preferred_element_type=jnp....  9.59 us
    convert_element_type x1, other arithmetic, shards(): (probs * (dprob - delta[..., None]) * softmax_scale).astype(jnp.bfloat16)  8.59 us
    all_gather x1, blocking collectives, shards(): lax.all_gather(own_lat.astype(jnp.bfloat16), 'head', axis=0, tiled=True)  8.41 us
  transfers between devices with their start and end apart: 15, of which 5 were waited for; matrix products, arithmetic and copies ran while one was open for 20% of the time, Pallas kernels for 0%

commit v1 on v0

--- a/solution.py
+++ b/solution.py
@@ -75,7 +75,12 @@
         own_lat = own_lat + got_lat
         own_rope = own_rope + got_rope
     latent_grad, key_rope_grad = (
-        lax.all_gather(own_lat.astype(jnp.bfloat16), "head", axis=0, tiled=True),
+        jnp.concatenate(
+            lax.all_to_all(
+                jnp.stack([own_lat.astype(jnp.bfloat16)] * lax.axis_size("head")), "head", 0, 0
+            ),
+            axis=0,
+        ),
         lax.all_gather(own_rope.astype(jnp.bfloat16), "head", axis=0, tiled=True),
     )
     proj_grad = lax.psum_scatter(

time: 201 us -> 216 us (1.075)
  waiting for transfers between devices: 51.3 us -> 70.5 us
  blocking collectives: 16.6 us -> 8.16 us
  starting transfers between devices: 25.2 us -> 28.6 us
    reduce_scatter x1, waiting for transfers between devices: 7.45 us -> 18.6 us  [shards(): lax.psum_scatter(blocks_rope, 'head', scatter_dimension=1, tiled=True)]
    reduce_scatter x1, waiting for transfers between devices: 19.6 us -> 28.2 us  [shards(): lax.psum_scatter(blocks_lat, 'head', scatter_dimension=1, tiled=True)]
    all_gather x1 -> x0, blocking collectives: 8.41 us -> none  [shards(): lax.all_gather(own_lat.astype(jnp.bfloat16), 'head', axis=0, tiled=True)]
    all_to_all x0 -> x1, starting transfers between devices: none -> 3.33 us  [shards(): lax.all_to_all(jnp.stack([own_lat.astype(jnp.bfloat16)] * lax.axis_size('...]
  transfers between devices with their start and end apart: 15 -> 16, of which waited for: 5 -> 4; matrix products, arithmetic and copies ran while one was open for 20% -> 19% of each run, Pallas kernels for 0% -> 0%
where the time goes in v1:
time: 216 us; the launch traced here: 215 us
  waiting for transfers between devices  70.5 us (33%)
  matrix products  61.2 us (28%)
  starting transfers between devices  28.6 us (13%)
  local copies, waits for them, and re-layouts  19.3 us (9%)
  between operations  14 us (6%)
  other arithmetic  13.1 us (6%)
  blocking collectives  8.16 us (4%)
    reduce_scatter x1, waiting for transfers between devices, shards(): lax.psum_scatter(blocks_lat, 'head', scatter_dimension=1, tiled=True)  28.2 us
    ppermute x12, starting transfers between devices, passed_along(): return lax.ppermute(array, axis, pairs)  25.1 us
    reduce_scatter x1, waiting for transfers between devices, shards(): lax.psum_scatter(lax.dot_general(latent_grad, inputs, (((0,), (0,)), ((),...  22.7 us
    reduce_scatter x1, waiting for transfers between devices, shards(): lax.psum_scatter(blocks_rope, 'head', scatter_dimension=1, tiled=True)  18.6 us
    unnamed x17, local copies, waits for them, and re-layouts  16.2 us
    dot_general x1, matrix products, shards(): jnp.einsum('thj,kj->thk', out_grad, keys_lat, preferred_element_type=jnp....  10.1 us
    dot_general x1, matrix products, shards(): jnp.einsum('thj,kj->thk', q_latent, keys_lat, preferred_element_type=jnp....  9.59 us
    convert_element_type x1, other arithmetic, shards(): (probs * (dprob - delta[..., None]) * softmax_scale).astype(jnp.bfloat16)  8.71 us
  transfers between devices with their start and end apart: 16, of which 4 were waited for; matrix products, arithmetic and copies ran while one was open for 19% of the time, Pallas kernels for 0%

profile of v1, /device:TPU:0, one launch (start us, length us, event | category | flops | bytes accessed | tf_op | source)
XLA Modules:
  0.0 214.8 jit_solution(594858309032413089)
XLA Ops:
  7.2 4.5 %collective-permute-start.3 = (bf16[128,64]{0,1:T(8,128)(2,1)}, bf16[128,64]{0,1:T(8,128)(2,1)S(1)}, u32[]{:S(2)}, u32[]{:S(2)}) collective-permute-start(bf16[128,64]{0,1:T(8,128)(2,1)} %param.10), channel_id=1, source_target_pairs={{0,12},{4,16},{8,20},{12,24},{16,28},{1,13},{5,17},{9,21},{13,25},... | collective-permute-start | bytes 49160 | tf_op jit(solution)/shard_map/ppermute | solution.py:13
  11.8 3.5 %collective-permute-start.4 = (bf16[128,64]{0,1:T(8,128)(2,1)}, bf16[128,64]{0,1:T(8,128)(2,1)S(1)}, u32[]{:S(2)}, u32[]{:S(2)}) collective-permute-start(bf16[128,64]{0,1:T(8,128)(2,1)} %param.10), channel_id=1, source_target_pairs={{0,8},{4,12},{8,16},{12,20},{16,24},{20,28},{1,9},{5,13},{9,17},{1... | collective-permute-start | bytes 49160 | tf_op jit(solution)/shard_map/ppermute | solution.py:13
  15.3 3.3 %collective-permute-start.5 = (bf16[128,64]{0,1:T(8,128)(2,1)}, bf16[128,64]{0,1:T(8,128)(2,1)S(1)}, u32[]{:S(2)}, u32[]{:S(2)}) collective-permute-start(bf16[128,64]{0,1:T(8,128)(2,1)} %param.10), channel_id=1, source_target_pairs={{0,4},{4,8},{8,12},{12,16},{16,20},{20,24},{24,28},{1,5},{5,9},{9,... | collective-permute-start | bytes 49160 | tf_op jit(solution)/shard_map/ppermute | solution.py:13
  18.6 1.8 collective-permute-start
  20.4 1.7 collective-permute-start.1
  22.1 0.8 pad_dynamic-slice_fusion
  22.9 0.8 dynamic_slice.7
  23.7 0.2 fusion.34
  23.9 1.3 copy.27
  25.2 2.3 %collective-permute-start.2 = (bf16[128,512]{1,0:T(8,128)(2,1)}, bf16[128,512]{1,0:T(8,128)(2,1)S(1)}, u32[]{:S(2)}, u32[]{:S(2)}) collective-permute-start(bf16[128,512]{1,0:T(8,128)(2,1)} %param.9), channel_id=1, source_target_pairs={{0,4},{4,8},{8,12},{12,16},{16,20},{20,24},{24,28},{1,5},{5,9},{9,... | collective-permute-start | bytes 393224 | tf_op jit(solution)/shard_map/ppermute | solution.py:13
  27.5 2.0 fusion.41
  29.5 9.6 %fusion.7 = (f32[128,32]{0,1:T(8,128)S(1)}, f32[512,128,32]{1,0,2:T(8,128)S(1)}) fusion(pred[128,512]{0,1:T(8,128)(4,1)S(1)} %fusion.34, f32[512,128,32]{1,0,2:T(8,128)S(1)} %fusion.41, bf16[128,32,512]{2,1,0:T(8,128)(2,1)} %param.7, bf16[128,512]{1,0:T(8,128)(2,1)S(1)} %copy-done.3, bf16[128,512]{1,0:T(8,128)(2,1)S(1)} %collective-permute-done.2, ...), kind=kOutput, calls=%fused_computation.14 | convolution fusion | flops 2157965312 | bytes 21577728 | tf_op jit(solution)/shard_map/thj,kj->thk/dot_general | solution.py:42
  39.1 1.6 fusion.9
  40.8 3.6 %copy-done.5 = bf16[128,32,512]{2,1,0:T(8,128)(2,1)S(1)} copy-done((bf16[128,32,512]{2,1,0:T(8,128)(2,1)S(1)}, bf16[128,32,512]{2,1,0:T(8,128)(2,1)}, u32[]{:S(2)}) %copy-start.5) | copy-done | bytes 4194328
  44.4 7.6 %fusion.22 = f32[512,512]{1,0:T(8,128)S(1)} fusion(bf16[128,32,512]{2,1,0:T(8,128)(2,1)S(1)} %copy-done.5, f32[512,128,32]{1,0,2:T(8,128)S(1)} %get-tuple-element.22, f32[128,32]{0,1:T(8,128)S(1)} %fusion.9, f32[128,32]{0,1:T(8,128)S(1)} %get-tuple-element.21, pred[128,512]{0,1:T(8,128)(4,1)S(1)} %fusion.34), kind=kOutput, calls=%fused_computation.28 | convolution fusion | flops 2155872256 | bytes 13729792 | tf_op jit(solution)/shard_map/thk,thj->kj/dot_general | solution.py:61
  52.0 7.4 %multiply_reduce_fusion = f32[128,32]{0,1:T(8,128)S(1)} fusion(bf16[128,32,512]{2,1,0:T(8,128)(2,1)S(1)} %copy-done.5, bf16[128,512]{1,0:T(8,128)(2,1)S(1)} %copy-done.3, bf16[128,512]{1,0:T(8,128)(2,1)S(1)} %collective-permute-done.2, bf16[128,512]{1,0:T(8,128)(2,1)S(1)} %collective-permute-done.1, bf16[128,512]{1,0:T(8,128)(2,1)S(1)} %collective-permute-done, ...), kind=kOutput, calls=%fused_computation.11 | convolution fusion | flops 2164256768 | bytes 13221888 | tf_op jit(solution)/shard_map/thk,kj->thj/dot_general | solution.py:50
  59.4 10.1 %fusion.6 = (bf16[128,32,512]{0,2,1:T(8,128)(2,1)S(1)}, f32[512,128,32]{1,0,2:T(8,128)}) fusion(f32[128,32]{0,1:T(8,128)S(1)} %multiply_reduce_fusion, f32[128,32]{0,1:T(8,128)S(1)} %fusion.9, f32[128,32]{0,1:T(8,128)S(1)} %get-tuple-element.21, f32[512,128,32]{1,0,2:T(8,128)S(1)} %get-tuple-element.22, pred[128,512]{0,1:T(8,128)(4,1)S(1)} %fusion.34, ...), kind=kOutput, calls=%fused_computation.9 | convolution fusion | flops 2164260864 | bytes 25804800 | tf_op jit(solution)/shard_map/thj,kj->thk/dot_general | solution.py:52
  69.6 2.0 copy-done.2
  71.6 8.3 %fusion.30 = f32[512,512]{1,0:T(8,128)} fusion(f32[512,512]{1,0:T(8,128)S(1)} %fusion.22, bf16[128,32,512]{0,2,1:T(8,128)(2,1)S(1)} %get-tuple-element.23, bf16[128,32,512]{2,1,0:T(8,128)(2,1)} %param.7), kind=kOutput, calls=%fused_computation.30 | convolution fusion | flops 2147745792 | bytes 10485760 | tf_op jit(solution)/shard_map/thk,thj->kj/dot_general | solution.py:59
  79.9 0.2 fusion.36
  80.1 28.2 %reduce-scatter.4.cloned.1.call-done = f32[4,32,512]{2,1,0:T(8,128)} async-done(((f32[4,128,512]{2,1,0:T(8,128)}), f32[4,32,512]{2,1,0:T(8,128)}) %reduce-scatter.4.cloned.1.call-update) | async-done | bytes 262160 | tf_op jit(solution)/shard_map/reduce_scatter | solution.py:66
  108.3 0.9 slice_bitcast_fusion.2
  109.2 1.3 collective-permute-start.6
  110.5 1.3 collective-permute-start.7
  111.8 1.3 collective-permute-start.8
  113.1 8.7 %fusion.2 = bf16[512,32,128]{2,0,1:T(8,128)(2,1)} fusion(f32[512,128,32]{1,0,2:T(8,128)} %get-tuple-element.24, f32[512,128,32]{1,0,2:T(8,128)} %copy-done.1, f32[32,128]{1,0:T(8,128)S(1)} %bitcast.123, f32[32,128]{1,0:T(8,128)S(1)} %bitcast.122, f32[32,128]{1,0:T(8,128)S(1)} %bitcast.121, pred[512,128]{1,0:T(8,128)(4,1)S(1)} %fusion.36), kind=kLoop, calls=%fused_computation.3 | loop fusion | flops 14680064 | bytes 21086208 | tf_op jit(solution)/shard_map/convert_element_type | solution.py:53
  121.8 0.9 fusion.40
  122.7 0.7 stack.2
  123.4 3.3 %all-to-all-start = ((bf16[4,32,512]{2,1,0:T(8,128)(2,1)}), bf16[4,32,512]{2,1,0:T(8,128)(2,1)S(1)}, u32[]{:S(2)}, u32[]{:S(2)}) async-start(bf16[4,32,512]{2,1,0:T(8,128)(2,1)} %stack.2), calls=%async_computation.1 | async-start | bytes 262144 | tf_op jit(solution)/shard_map/all_to_all | solution.py:79
  126.7 0.0 reduce-scatter.6.cloned.1.call-start
  126.8 4.1 %convolution_bitcast_fusion = f32[4,128,64]{2,1,0:T(8,128)} fusion(bf16[4,128,32,128]{3,1,0,2:T(8,128)(2,1)} %bitcast.114, bf16[128,32,64,1]{0,2,3,1:T(8,128)(2,1)S(1)} %bitcast.116), kind=kOutput, calls=%fused_computation.32 | convolution fusion | flops 268435456 | bytes 4849664 | tf_op jit(solution)/shard_map/thk,thr->kr/dot_general | solution.py:62
  130.9 0.0 reduce-scatter.8.cloned.1.call-start
  130.9 0.9 all-to-all-done
  131.9 2.4 %fusion.50 = f32[512,1792]{1,0:T(8,128)} fusion(bf16[128,512]{1,0:T(8,128)(2,1)S(1)} %bitcast.118, bf16[128,1792]{1,0:T(8,128)(2,1)S(1)} %copy-done), kind=kOutput, calls=%fused_computation.64 | convolution fusion | flops 234881024 | bytes 4259840 | tf_op jit(solution)/shard_map/dot_general | solution.py:87
  134.4 6.5 %convolution_convert_fusion = bf16[128,32,512]{2,0,1:T(8,128)(2,1)} fusion(bf16[128,32,512]{0,2,1:T(8,128)(2,1)} %copy-done.2, bf16[128,512]{1,0:T(8,128)(2,1)S(1)} %copy-done.3, bf16[128,512]{1,0:T(8,128)(2,1)S(1)} %collective-permute-done.2, bf16[128,512]{1,0:T(8,128)(2,1)S(1)} %collective-permute-done.1, bf16[128,512]{1,0:T(8,128)(2,1)S(1)} %collective-permute-done), kind=kOutput, calls=%fused_computation.25 | convolution fusion | flops 2151677952 | bytes 8912896 | tf_op jit(solution)/shard_map/thk,kj->thj/dot_general | solution.py:54
  140.9 18.6 %reduce-scatter.6.cloned.1.call-done = f32[4,32,64]{2,1,0:T(8,128)} async-done(((f32[4,128,64]{2,1,0:T(8,128)}), f32[4,32,64]{2,1,0:T(8,128)}) %reduce-scatter.6.cloned.1.call-update) | async-done | bytes 32784 | tf_op jit(solution)/shard_map/reduce_scatter | solution.py:67
  159.5 0.8 slice_bitcast_fusion.6
  160.2 1.3 collective-permute-start.10
  161.5 1.3 collective-permute-start.11
  162.8 1.6 collective-permute-start.9
  164.4 3.0 %convolution_convert_fusion.1 = bf16[128,32,64]{0,2,1:T(8,128)(2,1)S(1)} fusion(bf16[128,32,512]{0,2,1:T(8,128)(2,1)} %copy-done.2, bf16[128,64]{0,1:T(8,128)(2,1)S(1)} %copy-done.4, bf16[128,64]{0,1:T(8,128)(2,1)S(1)} %collective-permute-done.5, bf16[128,64]{0,1:T(8,128)(2,1)S(1)} %collective-permute-done.4, bf16[128,64]{0,1:T(8,128)(2,1)S(1)} %collective-permute-done.3), kind=kOutput, calls=%fused_computation.31 | convolution fusion | flops 268959744 | bytes 4784128 | tf_op jit(solution)/shard_map/thk,kr->thr/dot_general | solution.py:57
  167.4 6.9 %copy.36 = bf16[128,32,512]{2,1,0:T(8,128)(2,1)} copy(bf16[128,32,512]{2,0,1:T(8,128)(2,1)} %convolution_convert_fusion) | data formatting | bytes 8388608
  174.3 1.0 copy.37
  175.3 0.7 fusion.45
  176.0 8.2 %all_gather.3 = bf16[128,64]{1,0:T(8,128)(2,1)S(1)} all-gather(bf16[32,64]{1,0:T(8,128)(2,1)S(1)} %fusion.45), channel_id=1, replica_groups=mesh['ctx'=8,'head'=4] {'head'}, dimensions={0}, use_global_device_ids=true | all-gather | bytes 20480 | tf_op jit(solution)/shard_map/all_gather | solution.py:84
  184.2 0.7 copy.38
  184.9 22.7 %reduce-scatter.8.cloned.1.call-done = f32[64,1792]{1,0:T(8,128)} async-done(((f32[512,1792]{1,0:T(8,128)}), f32[64,1792]{1,0:T(8,128)}) %reduce-scatter.8.cloned.1.call-update) | async-done | bytes 458768 | tf_op jit(solution)/shard_map/reduce_scatter | solution.py:86
  207.6 0.7 copy.66
  (26 shorter events, 0.1 us)
Async XLA Ops:
  7.2 124.7 %copy-start = (bf16[128,1792]{1,0:T(8,128)(2,1)S(1)}, bf16[128,1792]{1,0:T(8,128)(2,1)}, u32[]{:S(2)}) copy-start(bf16[128,1792]{1,0:T(8,128)(2,1)} %param.12) | copy-start | bytes 1376260
  7.2 22.3 %copy-start.3 = (bf16[128,512]{1,0:T(8,128)(2,1)S(1)}, bf16[128,512]{1,0:T(8,128)(2,1)}, u32[]{:S(2)}) copy-start(bf16[128,512]{1,0:T(8,128)(2,1)} %param.9) | copy-start | bytes 393220
  7.2 101.1 %reduce-scatter.4.cloned.1.call-start = ((), (), s32[]{:S(2)}) async-start(), calls=%async_computation.4 | async-start | bytes 1310720 | tf_op jit(solution)/shard_map/reduce_scatter | solution.py:66
  7.2 18.0 %collective-permute-start.3 = (bf16[128,64]{0,1:T(8,128)(2,1)}, bf16[128,64]{0,1:T(8,128)(2,1)S(1)}, u32[]{:S(2)}, u32[]{:S(2)}) collective-permute-start(bf16[128,64]{0,1:T(8,128)(2,1)} %param.10), channel_id=1, source_target_pairs={{0,12},{4,16},{8,20},{12,24},{16,28},{1,13},{5,17},{9,21},{13,25},... | collective-permute-start | bytes 49160 | tf_op jit(solution)/shard_map/ppermute | solution.py:13
  11.8 15.7 %collective-permute-start.4 = (bf16[128,64]{0,1:T(8,128)(2,1)}, bf16[128,64]{0,1:T(8,128)(2,1)S(1)}, u32[]{:S(2)}, u32[]{:S(2)}) collective-permute-start(bf16[128,64]{0,1:T(8,128)(2,1)} %param.10), channel_id=1, source_target_pairs={{0,8},{4,12},{8,16},{12,20},{16,24},{20,28},{1,9},{5,13},{9,17},{1... | collective-permute-start | bytes 49160 | tf_op jit(solution)/shard_map/ppermute | solution.py:13
  15.3 12.2 %collective-permute-start.5 = (bf16[128,64]{0,1:T(8,128)(2,1)}, bf16[128,64]{0,1:T(8,128)(2,1)S(1)}, u32[]{:S(2)}, u32[]{:S(2)}) collective-permute-start(bf16[128,64]{0,1:T(8,128)(2,1)} %param.10), channel_id=1, source_target_pairs={{0,4},{4,8},{8,12},{12,16},{16,20},{20,24},{24,28},{1,5},{5,9},{9,... | collective-permute-start | bytes 49160 | tf_op jit(solution)/shard_map/ppermute | solution.py:13
  18.6 10.9 %collective-permute-start = (bf16[128,512]{1,0:T(8,128)(2,1)}, bf16[128,512]{1,0:T(8,128)(2,1)S(1)}, u32[]{:S(2)}, u32[]{:S(2)}) collective-permute-start(bf16[128,512]{1,0:T(8,128)(2,1)} %param.9), channel_id=1, source_target_pairs={{0,12},{4,16},{8,20},{12,24},{16,28},{1,13},{5,17},{9,21},{13,25},... | collective-permute-start | bytes 393224 | tf_op jit(solution)/shard_map/ppermute | solution.py:13
  20.4 9.1 %collective-permute-start.1 = (bf16[128,512]{1,0:T(8,128)(2,1)}, bf16[128,512]{1,0:T(8,128)(2,1)S(1)}, u32[]{:S(2)}, u32[]{:S(2)}) collective-permute-start(bf16[128,512]{1,0:T(8,128)(2,1)} %param.9), channel_id=1, source_target_pairs={{0,8},{4,12},{8,16},{12,20},{16,24},{20,28},{1,9},{5,13},{9,17},{1... | collective-permute-start | bytes 393224 | tf_op jit(solution)/shard_map/ppermute | solution.py:13
  25.2 4.3 %collective-permute-start.2 = (bf16[128,512]{1,0:T(8,128)(2,1)}, bf16[128,512]{1,0:T(8,128)(2,1)S(1)}, u32[]{:S(2)}, u32[]{:S(2)}) collective-permute-start(bf16[128,512]{1,0:T(8,128)(2,1)} %param.9), channel_id=1, source_target_pairs={{0,4},{4,8},{8,12},{12,16},{16,20},{20,24},{24,28},{1,5},{5,9},{9,... | collective-permute-start | bytes 393224 | tf_op jit(solution)/shard_map/ppermute | solution.py:13
  39.1 20.3 %copy-start.1 = (f32[512,128,32]{1,0,2:T(8,128)}, f32[512,128,32]{1,0,2:T(8,128)S(1)}, u32[]{:S(2)}) copy-start(f32[512,128,32]{1,0,2:T(8,128)S(1)} %get-tuple-element.22) | copy-start | bytes 25165828
  39.1 5.2 %copy-start.5 = (bf16[128,32,512]{2,1,0:T(8,128)(2,1)S(1)}, bf16[128,32,512]{2,1,0:T(8,128)(2,1)}, u32[]{:S(2)}) copy-start(bf16[128,32,512]{2,1,0:T(8,128)(2,1)} %param.11) | copy-start | bytes 12582916
  69.6 2.0 copy-start.2
  109.2 12.6 %collective-permute-start.6 = (f32[32,512]{1,0:T(8,128)S(1)}, f32[32,512]{1,0:T(8,128)S(1)}, u32[]{:S(2)}, u32[]{:S(2)}) collective-permute-start(f32[32,512]{1,0:T(8,128)S(1)} %get-tuple-element.15), channel_id=1, source_target_pairs={{4,0},{8,4},{12,8},{16,12},{20,16},{24,20},{28,24},{5,1},{9,5},{13... | collective-permute-start | bytes 196616 | tf_op jit(solution)/shard_map/ppermute | solution.py:13
  110.5 11.3 %collective-permute-start.7 = (f32[32,512]{1,0:T(8,128)S(1)}, f32[32,512]{1,0:T(8,128)S(1)}, u32[]{:S(2)}, u32[]{:S(2)}) collective-permute-start(f32[32,512]{1,0:T(8,128)S(1)} %get-tuple-element.17), channel_id=1, source_target_pairs={{8,0},{12,4},{16,8},{20,12},{24,16},{28,20},{9,1},{13,5},{17,9},{2... | collective-permute-start | bytes 196616 | tf_op jit(solution)/shard_map/ppermute | solution.py:13
  111.8 10.0 %collective-permute-start.8 = (f32[32,512]{1,0:T(8,128)S(1)}, f32[32,512]{1,0:T(8,128)S(1)}, u32[]{:S(2)}, u32[]{:S(2)}) collective-permute-start(f32[32,512]{1,0:T(8,128)S(1)} %get-tuple-element.16), channel_id=1, source_target_pairs={{12,0},{16,4},{20,8},{24,12},{28,16},{13,1},{17,5},{21,9},{25,13},... | collective-permute-start | bytes 196616 | tf_op jit(solution)/shard_map/ppermute | solution.py:13
  123.4 8.5 %all-to-all-start = ((bf16[4,32,512]{2,1,0:T(8,128)(2,1)}), bf16[4,32,512]{2,1,0:T(8,128)(2,1)S(1)}, u32[]{:S(2)}, u32[]{:S(2)}) async-start(bf16[4,32,512]{2,1,0:T(8,128)(2,1)} %stack.2), calls=%async_computation.1 | async-start | bytes 262144 | tf_op jit(solution)/shard_map/all_to_all | solution.py:79
  126.7 32.8 %reduce-scatter.6.cloned.1.call-start = ((), (), s32[]{:S(2)}) async-start(), calls=%async_computation.5 | async-start | bytes 327680 | tf_op jit(solution)/shard_map/reduce_scatter | solution.py:67
  130.9 76.7 %reduce-scatter.8.cloned.1.call-start = ((), (), s32[]{:S(2)}) async-start(), calls=%async_computation.6 | async-start | bytes 4128768 | tf_op jit(solution)/shard_map/reduce_scatter | solution.py:86
  131.9 32.5 %copy-start.4 = (bf16[128,64]{0,1:T(8,128)(2,1)S(1)}, bf16[128,64]{0,1:T(8,128)(2,1)}, u32[]{:S(2)}) copy-start(bf16[128,64]{0,1:T(8,128)(2,1)} %param.10) | copy-start | bytes 49156
  160.2 15.1 %collective-permute-start.10 = (f32[32,64]{1,0:T(8,128)S(1)}, f32[32,64]{1,0:T(8,128)S(1)}, u32[]{:S(2)}, u32[]{:S(2)}) collective-permute-start(f32[32,64]{1,0:T(8,128)S(1)} %get-tuple-element.20), channel_id=1, source_target_pairs={{8,0},{12,4},{16,8},{20,12},{24,16},{28,20},{9,1},{13,5},{17,9},{2... | collective-permute-start | bytes 24584 | tf_op jit(solution)/shard_map/ppermute | solution.py:13
  161.5 13.8 %collective-permute-start.11 = (f32[32,64]{1,0:T(8,128)S(1)}, f32[32,64]{1,0:T(8,128)S(1)}, u32[]{:S(2)}, u32[]{:S(2)}) collective-permute-start(f32[32,64]{1,0:T(8,128)S(1)} %get-tuple-element.19), channel_id=1, source_target_pairs={{12,0},{16,4},{20,8},{24,12},{28,16},{13,1},{17,5},{21,9},{25,13},... | collective-permute-start | bytes 24584 | tf_op jit(solution)/shard_map/ppermute | solution.py:13
  162.8 12.5 %collective-permute-start.9 = (f32[32,64]{1,0:T(8,128)S(1)}, f32[32,64]{1,0:T(8,128)S(1)}, u32[]{:S(2)}, u32[]{:S(2)}) collective-permute-start(f32[32,64]{1,0:T(8,128)S(1)} %get-tuple-element.18), channel_id=1, source_target_pairs={{4,0},{8,4},{12,8},{16,12},{20,16},{24,20},{28,24},{5,1},{9,5},{13... | collective-permute-start | bytes 24584 | tf_op jit(solution)/shard_map/ppermute | solution.py:13
Sparse Core Ops, SparseCore 0:
  80.0 28.2 reduce-scatter.3
  131.0 28.4 reduce-scatter.5
  162.4 45.2 reduce-scatter.7
